TPU v7x, 32 devices: a whole 2x2x4 slice. The times are simulated.
32 devices in a mesh: tok: 4 (over y, x), col: 8 (over z, core).
Axes of the slice: x: 2, y: 2, z: 4, core: 2. Of those that a mesh axis runs over, the one named last changes fastest.
Arguments:
- row_bank: bfloat16 [16384, 8192], P(None, 'col'), may hold values from -50 to 50
- token_ids: int32 [6144], P('tok'), may hold values from 0 to 16383
- sign_flips: int32 [8192], P('col'), may hold values from -1 to 1, as said below
- damping: float32 [1], replicated, may hold values from 0.1 to 1
Outputs:
- hessian: float32 [8192, 8192], P('tok', 'col')
Inputs may be any that keep to these rules, and one draw needn't show every extreme that they name: `sign_flips`: each entry is -1 or 1.
All inputs are finite; a program needn't handle non-finite values.
Results may differ from a plain program's by a relative error of at most 0.0003.
The roundings to bfloat16 on the way count: a program that leaves them out, or rounds other values in their place, can miss the bound.
Values may be sent and summed in bfloat16 or wider, within the bound.
A program may use at most 192 MiB of HBM per device.

v0:
```python
import math

import jax
import jax.numpy as jnp
from jax import lax
from jax.sharding import PartitionSpec as P

D = 8192
BLOCK = 32


def hadamard(order):
    index_range = jnp.arange(order, dtype=jnp.int32)
    anded = jnp.bitwise_and(index_range[:, None], index_range[None, :])
    parity = jnp.zeros((order, order), jnp.int32)
    for bit_place in range(int(order).bit_length()):
        parity = parity + jnp.bitwise_and(jnp.right_shift(anded, bit_place), 1)
    return (1 - 2 * jnp.bitwise_and(parity, 1)).astype(jnp.bfloat16)


def shards(row_bank, token_ids, sign_flips, damping):
    col_width = row_bank.shape[1]
    col_count = lax.axis_size("col")
    tok_count = lax.axis_size("tok")
    tok_rows = token_ids.shape[0]
    groups = D // BLOCK
    scale = 1.0 / math.sqrt(D)
    inner_table = hadamard(BLOCK)
    outer_table = hadamard(groups)
    col_start = lax.axis_index("col") * col_width
    picked = jnp.take(row_bank, token_ids, axis=0) * sign_flips.astype(jnp.bfloat16)[None, :]
    shaped = picked.reshape(picked.shape[0], -1, BLOCK)
    turned = jnp.einsum("rab,bc->rac", shaped, inner_table, preferred_element_type=jnp.float32)
    half_turned = turned.astype(jnp.bfloat16).reshape(picked.shape)
    grouped = half_turned.reshape(col_count, tok_rows // col_count, col_width)
    block = lax.all_to_all(grouped, "col", split_axis=0, concat_axis=2, tiled=True)[0]
    shaped = block.reshape(block.shape[0], groups, BLOCK)
    turned = (
        jnp.einsum("rab,ac->rcb", shaped, outer_table, preferred_element_type=jnp.float32) * scale
    )
    finished = turned.astype(jnp.bfloat16).reshape(block.shape)[None]
    squares = jnp.sum(jnp.square(finished.astype(jnp.float32)))
    tokens_all = tok_rows * tok_count
    square_sum = lax.psum(squares, ("tok", "col"))
    mean_diag = square_sum / tokens_all / D
    flat = lax.all_gather(finished, "col", axis=1, tiled=True).reshape(-1, D)
    own_cols = lax.dynamic_slice_in_dim(flat, col_start, col_width, 1)
    partial_sum = lax.dot_general(
        flat, own_cols, (((0,), (0,)), ((), ())), preferred_element_type=jnp.float32
    )
    gram_block = lax.psum_scatter(partial_sum, "tok", scatter_dimension=0, tiled=True) / tokens_all
    block_rows = gram_block.shape[0]
    row_index = lax.axis_index("tok") * block_rows + lax.broadcasted_iota(
        jnp.int32, gram_block.shape, 0
    )
    col_index = col_start + lax.broadcasted_iota(jnp.int32, gram_block.shape, 1)
    on_diag = (row_index == col_index).astype(jnp.float32)
    return gram_block + damping[0] * mean_diag * on_diag


def solution(mesh):
    in_specs = (P(None, "col"), P("tok"), P("col"), P())
    out_specs = P("tok", "col")
    return jax.shard_map(shards, mesh=mesh, in_specs=in_specs, out_specs=out_specs, check_vma=False)
```

profile of v0, /device:TPU:0, one launch (start us, length us, event | category | flops | bytes accessed | tf_op | source)
XLA Modules:
  0.0 692.3 jit_solution(12637017353230241267)
XLA Ops:
  6.5 0.0 all-gather.2.cloned.1.call-start
  6.5 0.7 compare_select_fusion
  7.2 0.7 compare_and_fusion
  7.9 11.4 %gather_fusion = bf16[1536,1024]{1,0:T(8,128)(2,1)S(1)} fusion(bf16[16384,1024]{1,0:T(8,128)(2,1)} %param.4, s32[2048]{0:T(1024)S(1)} %pad_clamp_fusion), kind=kCustom, calls=%fused_computation | custom fusion | bytes 6297600 | tf_op jit(solution)/shard_map/jit(_take)/gather | solution.py:31
  19.4 0.0 copy-start
  19.4 2.9 copy.10
  22.3 0.0 copy-done
  22.3 0.1 mul.40
  22.4 2.9 convolution_convert_fusion
  25.3 4.4 reshape_reshape.3
  29.8 5.7 copy.11
  35.5 77.8 %all_to_all.15 = bf16[8,192,1024]{2,1,0:T(8,128)(2,1)} all-to-all(bf16[8,192,1024]{2,1,0:T(8,128)(2,1)S(1)} %copy.11), channel_id=1, replica_groups=mesh['tok'=4,'col'=8] {'col'}, dimensions={0} | all-to-all | bytes 6291456 | tf_op jit(solution)/shard_map/all_to_all | solution.py:36
  113.3 6.1 copy.12
  119.4 7.5 %multiply_reduce_fusion = (f32[]{:T(128)}, bf16[192,256,32]{1,0,2:T(8,128)(2,1)S(1)}) fusion(bf16[192,256,32]{0,2,1:T(8,128)(2,1)} %bitcast.28), kind=kOutput, calls=%fused_computation.4 | convolution fusion | flops 815202304 | bytes 6291460 | tf_op jit(solution)/shard_map/rab,ac->rcb/dot_general | solution.py:39
  126.9 5.5 copy.14
  132.4 6.0 copy.15
  138.4 0.0 all-gather.2.cloned.1.call-update
  138.4 0.2 reduce-scatter.2.cloned.1.call-start
  138.6 218.7 %all-gather.2.cloned.1.call-done = bf16[1,1536,8192]{2,1,0:T(8,128)(2,1)} async-done(((bf16[1,192,8192]{2,1,0:T(8,128)(2,1)}), bf16[1,1536,8192]{2,1,0:T(8,128)(2,1)}) %all-gather.2.cloned.1.call-update) | async-done | bytes 25165840 | tf_op jit(solution)/shard_map/all_gather | solution.py:46
  357.3 34.0 %fusion = f32[8192,1024]{1,0:T(8,128)} fusion(bf16[1,1536,8192]{2,1,0:T(8,128)(2,1)} %all-gather.2.cloned.1.call-done, s32[]{:T(128)S(6)} %select_n.15), kind=kOutput, calls=%fused_computation.1 | convolution fusion | flops 25769803776 | bytes 61865988 | tf_op jit(solution)/shard_map/dot_general | solution.py:48
  391.3 0.0 reduce-scatter.2.cloned.1.call-update
  392.0 39.7 %psum.7 = f32[]{:T(128)} all-reduce(f32[]{:T(128)} %get-tuple-element.5), channel_id=1, replica_groups=mesh['tok'=4,'col'=8] {'tok','col'}, use_global_device_ids=true, to_apply=%region_2.3 | all-reduce | flops 1 | bytes 8 | tf_op jit(solution)/shard_map/psum | solution.py:44
  432.3 247.0 %reduce-scatter.2.cloned.1.call-done = f32[2048,1024]{1,0:T(8,128)} async-done(((f32[8192,1024]{1,0:T(8,128)}), f32[2048,1024]{1,0:T(8,128)}) %reduce-scatter.2.cloned.1.call-update) | async-done | bytes 8388624 | tf_op jit(solution)/shard_map/reduce_scatter | solution.py:51
  679.3 6.2 select_add_fusion
  (4 shorter events, 0.0 us)
Async XLA Ops:
  6.5 350.8 %all-gather.2.cloned.1.call-start = ((), (), s32[]{:S(2)}) async-start(), calls=%async_computation.2 | async-start | bytes 28311552 | tf_op jit(solution)/shard_map/all_gather | solution.py:46
  19.4 2.9 copy-start
  138.4 540.9 %reduce-scatter.2.cloned.1.call-start = ((), (), s32[]{:S(2)}) async-start(), calls=%async_computation.3 | async-start | bytes 41943040 | tf_op jit(solution)/shard_map/reduce_scatter | solution.py:51
Sparse Core Ops, SparseCore 0:
  138.5 218.7 all-gather.1
  391.5 287.7 reduce-scatter.1
where the time goes:
time: 693 us; the launch traced here: 692 us
  waiting for transfers between devices  466 us (67%)
  blocking collectives  117 us (17%)
  matrix products  44.5 us (6%)
  local copies, waits for them, and re-layouts  42.1 us (6%)
  between operations  14.7 us (2%)
  other arithmetic  7.62 us (1%)
    reduce_scatter x1, waiting for transfers between devices, shards(): lax.psum_scatter(partial_sum, 'tok', scatter_dimension=0, tiled=True)  247 us
    all_gather x1, waiting for transfers between devices, shards(): flat = lax.all_gather(finished, 'col', axis=1, tiled=True).reshape(-1, D)  219 us
    all_to_all x1, blocking collectives, shards(): lax.all_to_all(grouped, 'col', split_axis=0, concat_axis=2, tiled=True)[0]  77.8 us
    psum x1, blocking collectives, shards(): square_sum = lax.psum(squares, ('tok', 'col'))  39.7 us
    dot_general x1, matrix products, shards(): lax.dot_general(flat, own_cols, (((0,), (0,)), ((), ())), preferred_eleme...  34 us
    gather x2, local copies, waits for them, and re-layouts, shards(): jnp.take(row_bank, token_ids, axis=0)  14.3 us
  transfers between devices with their start and end apart: 2, of which 2 were waited for; matrix products, arithmetic and copies ran while one was open for 0% of the time, Pallas kernels for 0%

commit v1 on v0

--- a/solution.py
+++ b/solution.py
@@ -1,12 +1,17 @@
+import functools
 import math
 
 import jax
 import jax.numpy as jnp
 from jax import lax
+from jax.experimental import pallas as pl
+from jax.experimental.pallas import tpu as pltpu
 from jax.sharding import PartitionSpec as P
 
 D = 8192
 BLOCK = 32
+LANES = 512
+MESH = pl.DeviceIdType.MESH
 
 
 def hadamard(order):
@@ -18,7 +23,377 @@
     return (1 - 2 * jnp.bitwise_and(parity, 1)).astype(jnp.bfloat16)
 
 
-def shards(row_bank, token_ids, sign_flips, damping):
+def fused_kernel(
+    planes, chunks, rows, piece, scale,
+    half_ref, table_ref,
+    gram_ref, gram_in_ref, square_ref, full_ref,
+    xbuf, tmp, rot, rxr, rxq, acc, squares,
+    part_send, part_recv, z_send, z_recv, r_send, r_recv, q_send, q_recv,
+    s_send, s_recv, g_send, g_recv, load_sem, out_sem,
+):
+    tok = lax.axis_index("tok")
+    col = lax.axis_index("col")
+    plane, core = col // 2, col % 2
+    mate = plane * 2 + (1 - core)
+    ypos, xpos = tok // 2, tok % 2
+    peers = {1: ypos * 2 + (1 - xpos), 2: (1 - ypos) * 2 + xpos, 3: 3 - tok}
+    wide = 2 * piece
+
+    barrier = pltpu.get_barrier_semaphore()
+    greet = [(tok, mate)]
+    for m in (1, 2, 3):
+        greet.append((peers[m], col))
+        greet.append((peers[m], mate))
+    for m in range(1, planes):
+        greet.append((tok, ((plane + m) % planes) * 2 + core))
+    for device in greet:
+        pl.semaphore_signal(barrier, inc=1, device_id=device, device_id_type=MESH)
+    pl.semaphore_wait(barrier, len(greet))
+
+    def part_copy(k):
+        return pltpu.make_async_remote_copy(
+            src_ref=half_ref.at[1 - core, k], dst_ref=full_ref.at[k, col],
+            send_sem=part_send.at[k], recv_sem=part_recv.at[k],
+            device_id=(tok, mate), device_id_type=MESH)
+
+    def part_arrival(k):
+        return pltpu.make_async_remote_copy(
+            src_ref=half_ref.at[1 - core, k], dst_ref=full_ref.at[k, mate],
+            send_sem=part_send.at[k], recv_sem=part_recv.at[k],
+            device_id=(tok, mate), device_id_type=MESH)
+
+    def z_copy(k, j, way, own=False):
+        source = half_ref.at[core, k] if own else full_ref.at[k, j]
+        return pltpu.make_async_remote_copy(
+            src_ref=source, dst_ref=full_ref.at[k, j],
+            send_sem=z_send.at[k, j, way], recv_sem=z_recv.at[k, j],
+            device_id=(tok, col + 2 - 4 * way), device_id_type=MESH)
+
+    can = {0: plane < planes - 1, 1: plane > 0}
+
+    def own_sends(k):
+        for way in (0, 1):
+            @pl.when(can[way])
+            def _():
+                z_copy(k, col, way, own=True).start()
+        part_arrival(k).wait_recv()
+        for way in (0, 1):
+            @pl.when(can[way])
+            def _():
+                z_copy(k, mate, way).start()
+
+    def row_copy(k, m):
+        return pltpu.make_async_remote_copy(
+            src_ref=rot.at[k, pl.ds(peers[m] * wide, wide)],
+            dst_ref=rxr.at[k, :, pl.ds(m * rows, rows)],
+            send_sem=r_send.at[k, m], recv_sem=r_recv.at[k, m],
+            device_id=(peers[m], col), device_id_type=MESH)
+
+    def col_copy(k, m):
+        return pltpu.make_async_remote_copy(
+            src_ref=rot.at[k, pl.ds(plane * wide, wide)],
+            dst_ref=rxq.at[k, :, pl.ds(m * rows, rows)],
+            send_sem=q_send.at[k, m], recv_sem=q_recv.at[k, m],
+            device_id=(peers[m], col), device_id_type=MESH)
+
+    def relay_copy(k):
+        odd = k % 2
+        target = peers[2] * (1 - odd) + peers[1] * odd
+        start = pl.multiple_of((1 + odd) * rows, rows)
+        return pltpu.make_async_remote_copy(
+            src_ref=rxq.at[k, :, pl.ds(start, rows)],
+            dst_ref=rxq.at[k, :, pl.ds(3 * rows, rows)],
+            send_sem=q_send.at[k, 3], recv_sem=q_recv.at[k, 3],
+            device_id=(target, col), device_id_type=MESH)
+
+    def z_stage(k):
+        for distance in range(1, planes):
+            for way, origin in ((0, plane - distance), (1, plane + distance)):
+                @pl.when((origin >= 0) & (origin < planes))
+                def _():
+                    for side in (0, 1):
+                        j = origin * 2 + (core if side == 0 else 1 - core)
+                        z_copy(k, j, way).wait_recv()
+
+                        @pl.when(can[way])
+                        def _():
+                            z_copy(k, j, way).start()
+            if distance == max(planes - 2, 1):
+                @pl.when(k + 1 < chunks)
+                def _():
+                    own_sends(k + 1)
+
+    def load_chunk(k):
+        copies = [pltpu.make_async_copy(half_ref.at[core, k], xbuf.at[col], load_sem.at[0])]
+        copies.append(pltpu.make_async_copy(full_ref.at[k, mate], xbuf.at[mate], load_sem.at[1]))
+        for m in range(1, planes):
+            other = ((plane + m) % planes) * 2
+            copies.append(pltpu.make_async_copy(
+                full_ref.at[k, pl.ds(other, 2)], xbuf.at[pl.ds(other, 2)], load_sem.at[1 + m]))
+        for copy in copies:
+            copy.start()
+        for copy in copies:
+            copy.wait()
+
+    groups = 2 * planes * piece
+
+    def rotate(k):
+        def product(j, carry):
+            block = xbuf[j].reshape(piece * rows, LANES)
+            out = jnp.dot(block, table_ref[...], preferred_element_type=jnp.float32)
+            tmp[pl.ds(j * piece, piece)] = out.reshape(piece, rows, LANES)
+            return carry
+
+        lax.fori_loop(0, 2 * planes, product, 0)
+
+        def butterfly(index, carry):
+            r = pl.multiple_of((index // (LANES // 128)) * 16, 16)
+            lane = pl.multiple_of((index % (LANES // 128)) * 128, 128)
+            values = [tmp[g, pl.ds(r, 16), pl.ds(lane, 128)] for g in range(groups)]
+            step = 1
+            while step < groups:
+                values = [
+                    values[g] + values[g + step] if g & step == 0 else values[g - step] - values[g]
+                    for g in range(groups)
+                ]
+                step *= 2
+            total = squares[0]
+            for g in range(groups):
+                rounded = (values[g] * scale).astype(jnp.bfloat16)
+                rot[k, g, pl.ds(r, 16), pl.ds(lane, 128)] = rounded
+                exact = rounded.astype(jnp.float32)
+                total = total + exact * exact
+            squares[0] = total
+            return carry
+
+        lax.fori_loop(0, (rows // 16) * (LANES // 128), butterfly, 0)
+        for f in range(wide):
+            rxr[k, f, pl.ds(0, rows)] = rot[k, tok * wide + f]
+            rxq[k, f, pl.ds(0, rows)] = rot[k, plane * wide + f]
+        for m in (1, 2):
+            col_copy(k, m).start()
+        for m in (1, 2, 3):
+            row_copy(k, m).start()
+
+    def arrivals(k):
+        odd = k % 2
+
+        @pl.when(odd == 0)
+        def _():
+            col_copy(k, 1).wait_recv()
+            relay_copy(k).start()
+            col_copy(k, 2).wait_recv()
+
+        @pl.when(odd == 1)
+        def _():
+            col_copy(k, 2).wait_recv()
+            relay_copy(k).start()
+            col_copy(k, 1).wait_recv()
+
+        for m in (1, 2, 3):
+            row_copy(k, m).wait_recv()
+        relay_copy(k).wait_recv()
+
+    def row_block(k, f):
+        left = rxr[k, f].T
+        start = pl.multiple_of(f * LANES, LANES)
+        for n in range(wide):
+            out = jnp.dot(left, rxq[k, n], preferred_element_type=jnp.float32)
+            acc[n // piece, pl.ds(start, LANES), pl.ds((n % piece) * LANES, LANES)] += out
+
+    def gram(k):
+        def body(f, carry):
+            row_block(k, f)
+            return carry
+
+        lax.fori_loop(0, wide, body, 0)
+
+    def gram_out(f):
+        span = pl.ds(pl.multiple_of(f * LANES, LANES), LANES)
+        return pltpu.make_async_remote_copy(
+            src_ref=acc.at[1 - core, span], dst_ref=gram_in_ref.at[span],
+            send_sem=g_send.at[f], recv_sem=g_recv.at[f],
+            device_id=(tok, mate), device_id_type=MESH)
+
+    def gram_keep(f):
+        span = pl.ds(pl.multiple_of(f * LANES, LANES), LANES)
+        return pltpu.make_async_copy(acc.at[core, span], gram_ref.at[span], out_sem.at[f])
+
+    def square_copy(m):
+        target = (tok, mate) if m == 4 else (peers[m % 4], col if m < 4 else mate)
+        return pltpu.make_async_remote_copy(
+            src_ref=squares.at[0], dst_ref=squares.at[m],
+            send_sem=s_send.at[m], recv_sem=s_recv.at[m],
+            device_id=target, device_id_type=MESH)
+
+    def send_part(k, carry):
+        part_copy(k).start()
+        return carry
+
+    lax.fori_loop(0, chunks, send_part, 0)
+    own_sends(0)
+    squares[0] = jnp.zeros((16, 128), jnp.float32)
+
+    def clear(index, carry):
+        start = pl.multiple_of((index % (acc.shape[1] // 64)) * 64, 64)
+        acc[index // (acc.shape[1] // 64), pl.ds(start, 64)] = jnp.zeros((64, acc.shape[2]), jnp.float32)
+        return carry
+
+    lax.fori_loop(0, acc.shape[0] * (acc.shape[1] // 64), clear, 0)
+
+    def step(k, carry):
+        z_stage(k)
+        load_chunk(k)
+        rotate(k)
+
+        @pl.when(k > 0)
+        def _():
+            arrivals(k - 1)
+            gram(k - 1)
+
+        return carry
+
+    lax.fori_loop(0, chunks, step, 0)
+    for m in range(1, 8):
+        square_copy(m).start()
+    last = chunks - 1
+    arrivals(last)
+
+    def final(f, carry):
+        row_block(last, f)
+
+        @pl.when(f > 0)
+        def _():
+            gram_out(f - 1).start()
+            gram_keep(f - 1).start()
+
+        return carry
+
+    lax.fori_loop(0, wide, final, 0)
+    for m in range(1, 8):
+        square_copy(m).wait()
+    sums = squares[0]
+    for m in range(1, 8):
+        sums = sums + squares[m]
+    square_ref[...] = sums
+    gram_out(wide - 1).start()
+    gram_keep(wide - 1).start()
+
+    def drain(k, carry):
+        part_copy(k).wait_send()
+        for j in range(2 * planes):
+            @pl.when(can[0] & (j // 2 <= plane))
+            def _():
+                z_copy(k, j, 0).wait_send()
+
+            @pl.when(can[1] & (j // 2 >= plane))
+            def _():
+                z_copy(k, j, 1).wait_send()
+        for m in (1, 2):
+            col_copy(k, m).wait_send()
+        relay_copy(k).wait_send()
+        for m in (1, 2, 3):
+            row_copy(k, m).wait_send()
+        return carry
+
+    lax.fori_loop(0, chunks, drain, 0)
+
+    def finish(f, carry):
+        gram_out(f).wait()
+        gram_keep(f).wait()
+        return carry
+
+    lax.fori_loop(0, wide, finish, 0)
+
+
+def fits(row_bank, token_ids):
+    col_width, tok_rows = row_bank.shape[1], token_ids.shape[0]
+    col_count, tok_count = lax.axis_size("col"), lax.axis_size("tok")
+    return (
+        col_width % LANES == 0
+        and tok_count == 4
+        and col_count % 2 == 0
+        and D // tok_count == 2 * col_width
+        and tok_rows % 256 == 0
+        and tok_rows * D * 6 + (D // tok_count) ** 2 * 4 <= 96 * 2**20
+    )
+
+
+def fused(row_bank, token_ids, sign_flips, damping):
+    col_width = row_bank.shape[1]
+    col_count = lax.axis_size("col")
+    tok_count = lax.axis_size("tok")
+    tok_rows = token_ids.shape[0]
+    planes = col_count // 2
+    own_rows = tok_rows // 2
+    rows = 64
+    chunks = own_rows // rows
+    piece = col_width // LANES
+    wide = 2 * piece
+    groups = D // LANES
+    spread = LANES // BLOCK
+    inner = jnp.kron(jnp.eye(spread, dtype=jnp.bfloat16), hadamard(BLOCK))
+    outer = jnp.kron(hadamard(spread), jnp.eye(BLOCK, dtype=jnp.bfloat16))
+    picked = jnp.take(row_bank, token_ids, axis=0) * sign_flips.astype(jnp.bfloat16)[None, :]
+    parts = []
+    for g in range(piece):
+        part = picked[:, g * LANES : (g + 1) * LANES]
+        part = jnp.dot(part, inner, preferred_element_type=jnp.float32).astype(jnp.bfloat16)
+        parts.append(part.reshape(2, chunks, rows, LANES))
+    half = jnp.stack(parts, axis=2)
+    any_space = pl.BlockSpec(memory_space=pl.ANY)
+    vmem = pl.BlockSpec(memory_space=pltpu.VMEM)
+    dma = pltpu.SemaphoreType.DMA
+    height = D // tok_count
+    gram, gram_in, squares, _ = pl.pallas_call(
+        functools.partial(fused_kernel, planes, chunks, rows, piece, 1.0 / math.sqrt(D)),
+        out_shape=(
+            jax.ShapeDtypeStruct((height, col_width), jnp.float32),
+            jax.ShapeDtypeStruct((height, col_width), jnp.float32),
+            jax.ShapeDtypeStruct((16, 128), jnp.float32),
+            jax.ShapeDtypeStruct((chunks, col_count, piece, rows, LANES), jnp.bfloat16),
+        ),
+        in_specs=[any_space, vmem],
+        out_specs=(any_space, any_space, vmem, any_space),
+        scratch_shapes=[
+            pltpu.VMEM((col_count, piece, rows, LANES), jnp.bfloat16),
+            pltpu.VMEM((groups, rows, LANES), jnp.float32),
+            pltpu.VMEM((chunks, groups, rows, LANES), jnp.bfloat16),
+            pltpu.VMEM((chunks, wide, 4 * rows, LANES), jnp.bfloat16),
+            pltpu.VMEM((chunks, wide, 4 * rows, LANES), jnp.bfloat16),
+            pltpu.VMEM((2, height, col_width), jnp.float32),
+            pltpu.VMEM((8, 16, 128), jnp.float32),
+            dma((chunks,)), dma((chunks,)),
+            dma((chunks, col_count, 2)), dma((chunks, col_count)),
+            dma((chunks, 4)), dma((chunks, 4)),
+            dma((chunks, 4)), dma((chunks, 4)),
+            dma((8,)), dma((8,)),
+            dma((wide,)), dma((wide,)),
+            dma((planes + 1,)), dma((wide,)),
+        ],
+        compiler_params=pltpu.CompilerParams(
+            collective_id=0, has_side_effects=True, vmem_limit_bytes=67043328
+        ),
+    )(half, outer)
+    tokens_all = tok_rows * tok_count
+    mean_diag = jnp.sum(squares) / tokens_all / D
+    gram_block = (gram + gram_in) / tokens_all
+    return damped(gram_block, damping, mean_diag)
+
+
+def damped(gram_block, damping, mean_diag):
+    block_rows, col_width = gram_block.shape
+    row_index = lax.axis_index("tok") * block_rows + lax.broadcasted_iota(
+        jnp.int32, gram_block.shape, 0
+    )
+    col_index = lax.axis_index("col") * col_width + lax.broadcasted_iota(
+        jnp.int32, gram_block.shape, 1
+    )
+    on_diag = (row_index == col_index).astype(jnp.float32)
+    return gram_block + damping[0] * mean_diag * on_diag
+
+
+def plain(row_bank, token_ids, sign_flips, damping):
     col_width = row_bank.shape[1]
     col_count = lax.axis_size("col")
     tok_count = lax.axis_size("tok")
@@ -49,13 +424,12 @@
         flat, own_cols, (((0,), (0,)), ((), ())), preferred_element_type=jnp.float32
     )
     gram_block = lax.psum_scatter(partial_sum, "tok", scatter_dimension=0, tiled=True) / tokens_all
-    block_rows = gram_block.shape[0]
-    row_index = lax.axis_index("tok") * block_rows + lax.broadcasted_iota(
-        jnp.int32, gram_block.shape, 0
-    )
-    col_index = col_start + lax.broadcasted_iota(jnp.int32, gram_block.shape, 1)
-    on_diag = (row_index == col_index).astype(jnp.float32)
-    return gram_block + damping[0] * mean_diag * on_diag
+    return damped(gram_block, damping, mean_diag)
+
+
+def shards(row_bank, token_ids, sign_flips, damping):
+    run = fused if fits(row_bank, token_ids) else plain
+    return run(row_bank, token_ids, sign_flips, damping)
 
 
 def solution(mesh):

time: 693 us -> 449 us (0.65)
  waiting for transfers between devices: 466 us -> 0 us
  Pallas kernels: 0 us -> 410 us
  blocking collectives: 117 us -> 0 us
  matrix products: 44.5 us -> 3.53 us
  local copies, waits for them, and re-layouts: 42.1 us -> 16.3 us
  between operations: 14.7 us -> 1.45 us
  other arithmetic: 7.62 us -> 16.7 us
    pallas_call x0 -> x1, Pallas kernels: none -> 410 us  [fused(): pl.pallas_call(functools.partial(fused_kernel, planes, chunks, rows, piec...]
    reduce_scatter x1 -> x0, waiting for transfers between devices: 247 us -> none  [shards(): lax.psum_scatter(partial_sum, 'tok', scatter_dimension=0, tiled=True)]
    all_gather x1 -> x0, waiting for transfers between devices: 219 us -> none  [shards(): flat = lax.all_gather(finished, 'col', axis=1, tiled=True).reshape(-1, D)]
    all_to_all x1 -> x0, blocking collectives: 77.8 us -> none  [shards(): lax.all_to_all(grouped, 'col', split_axis=0, concat_axis=2, tiled=True)[0]]
    dot_general x3 -> x2, matrix products: 44.5 us -> 3.53 us  [fused(): jnp.dot(part, inner, preferred_element_type=jnp.float32)]
    psum x1 -> x0, blocking collectives: 39.7 us -> none  [shards(): square_sum = lax.psum(squares, ('tok', 'col'))]
    another operation x3 -> x0, local copies, waits for them, and re-layouts: 16.1 us -> none  [the longest x2 10.1 us: shards(): grouped = half_turned.reshape(col_count, tok_rows // col_count, col_width)]
    gather x2 -> x1, local copies, waits for them, and re-layouts: 14.3 us -> 11.4 us  [fused(): jnp.take(row_bank, token_ids, axis=0)]
  transfers between devices with their start and end apart: 2 -> 0, of which waited for: 2 -> 0; matrix products, arithmetic and copies ran while one was open for 0% -> 0% of each run, Pallas kernels for 0% -> 0%
where the time goes in v1:
time: 449 us; the launch traced here: 448 us
  Pallas kernels  410 us (91%)
  other arithmetic  16.7 us (4%)
  local copies, waits for them, and re-layouts  16.3 us (4%)
    pallas_call x1, Pallas kernels, fused(): pl.pallas_call(functools.partial(fused_kernel, planes, chunks, rows, piec...  410 us
    gather x1, local copies, waits for them, and re-layouts, fused(): jnp.take(row_bank, token_ids, axis=0)  11.4 us
    add x1, other arithmetic, damped(): return gram_block + damping[0] * mean_diag * on_diag  10.1 us

profile of v1, /device:TPU:0, one launch (start us, length us, event | category | flops | bytes accessed | tf_op | source)
XLA Modules:
  0.0 447.9 jit_solution(12351240283767338970)
XLA Ops:
  0.0 0.7 compare_select_fusion
  0.7 0.0 copy-start.1
  0.7 0.0 copy-start.2
  0.7 11.4 %gather_fusion = bf16[1536,1024]{1,0:T(8,128)(2,1)S(1)} fusion(bf16[16384,1024]{1,0:T(8,128)(2,1)} %param.4, s32[2048]{0:T(1024)S(1)} %pad_clamp_fusion), kind=kCustom, calls=%fused_computation | custom fusion | bytes 6297600 | tf_op jit(solution)/shard_map/jit(_take)/gather | solution.py:337
  12.2 0.0 copy-done.1
  12.2 0.0 copy-done.2
  12.2 2.1 select_multiply_fusion
  14.4 0.2 broadcast_multiply_fusion.1
  14.6 2.1 mul.94
  16.6 0.0 copy-start
  16.7 2.5 convolution_convert_fusion.1
  19.2 0.0 copy-done
  19.2 1.0 convolution_convert_fusion
  20.2 1.9 pad_maximum_fusion.half_ref
  22.2 0.2 broadcast_multiply_fusion
  22.4 2.8 mul.99.table_ref
  25.2 410.0 %shard_map.46 = (f32[2048,1024]{1,0:T(8,128)}, f32[2048,1024]{1,0:T(8,128)}, f32[16,128]{1,0:T(8,128)}, bf16[12,8,2,64,512]{4,3,2,1,0:T(8,128)(2,1)}) custom-call(bf16[2,12,2,64,512]{4,3,2,1,0:T(8,128)(2,1)} %pad_maximum_fusion.half_ref, bf16[512,512]{1,0:T(8,128)(2,1)} %mul.99.table_ref), custom_call_target="tpu_custom_call" | custom-call | tf_op jit(solution)/shard_map/pallas_call | solution.py:348
  435.1 1.3 reduce_sum.9
  437.8 10.1 %select_add_fusion = f32[2048,1024]{1,0:T(8,128)} fusion(f32[2048,1024]{1,0:T(8,128)} %get-tuple-element.8, f32[2048,1024]{1,0:T(8,128)} %get-tuple-element.9, f32[]{:T(128)S(6)} %mul.102, s32[1024]{0:T(1024)S(1)} %iota_add_fusion.1, s32[2048]{0:T(1024)S(1)} %iota_add_fusion), kind=kLoop, calls=%fused_computation.1 | loop fusion | flops 10485760 | bytes 25178116 | tf_op jit(solution)/shard_map/add | solution.py:393
  (9 shorter events, 0.1 us)
Async XLA Ops:
  0.7 11.4 %copy-start.1 = (s32[1536]{0:T(1024)S(1)}, s32[1536]{0:T(1024)}, u32[]{:S(2)}) copy-start(s32[1536]{0:T(1024)} %param.5) | copy-start | bytes 18436
  0.7 11.5 %copy-start.2 = (s32[1024]{0:T(1024)S(1)}, s32[1024]{0:T(1024)}, u32[]{:S(2)}) copy-start(s32[1024]{0:T(1024)} %param.6) | copy-start | bytes 12292
  16.6 2.6 copy-start

commit v2 on v1

--- a/solution.py
+++ b/solution.py
@@ -3,6 +3,7 @@
 
 import jax
 import jax.numpy as jnp
+import numpy as np
 from jax import lax
 from jax.experimental import pallas as pl
 from jax.experimental.pallas import tpu as pltpu
@@ -21,6 +22,13 @@
     for bit_place in range(int(order).bit_length()):
         parity = parity + jnp.bitwise_and(jnp.right_shift(anded, bit_place), 1)
     return (1 - 2 * jnp.bitwise_and(parity, 1)).astype(jnp.bfloat16)
+
+
+def sylvester(order):
+    table = np.ones((1, 1))
+    while table.shape[0] < order:
+        table = np.block([[table, table], [table, -table]])
+    return table
 
 
 def fused_kernel(
@@ -106,22 +114,17 @@
             send_sem=q_send.at[k, 3], recv_sem=q_recv.at[k, 3],
             device_id=(target, col), device_id_type=MESH)
 
-    def z_stage(k):
-        for distance in range(1, planes):
-            for way, origin in ((0, plane - distance), (1, plane + distance)):
-                @pl.when((origin >= 0) & (origin < planes))
-                def _():
-                    for side in (0, 1):
-                        j = origin * 2 + (core if side == 0 else 1 - core)
-                        z_copy(k, j, way).wait_recv()
-
-                        @pl.when(can[way])
-                        def _():
-                            z_copy(k, j, way).start()
-            if distance == max(planes - 2, 1):
-                @pl.when(k + 1 < chunks)
-                def _():
-                    own_sends(k + 1)
+    def z_stage(k, distance):
+        for way, origin in ((0, plane - distance), (1, plane + distance)):
+            @pl.when((origin >= 0) & (origin < planes))
+            def _():
+                for side in (0, 1):
+                    j = origin * 2 + (core if side == 0 else 1 - core)
+                    z_copy(k, j, way).wait_recv()
+
+                    @pl.when(can[way])
+                    def _():
+                        z_copy(k, j, way).start()
 
     def load_chunk(k):
         copies = [pltpu.make_async_copy(half_ref.at[core, k], xbuf.at[col], load_sem.at[0])]
@@ -175,19 +178,28 @@
         for m in (1, 2, 3):
             row_copy(k, m).start()
 
+    def relay(k):
+        odd = k % 2
+
+        @pl.when(odd == 0)
+        def _():
+            col_copy(k, 1).wait_recv()
+
+        @pl.when(odd == 1)
+        def _():
+            col_copy(k, 2).wait_recv()
+
+        relay_copy(k).start()
+
     def arrivals(k):
         odd = k % 2
 
         @pl.when(odd == 0)
         def _():
-            col_copy(k, 1).wait_recv()
-            relay_copy(k).start()
             col_copy(k, 2).wait_recv()
 
         @pl.when(odd == 1)
         def _():
-            col_copy(k, 2).wait_recv()
-            relay_copy(k).start()
             col_copy(k, 1).wait_recv()
 
         for m in (1, 2, 3):
@@ -240,16 +252,38 @@
         return carry
 
     lax.fori_loop(0, acc.shape[0] * (acc.shape[1] // 64), clear, 0)
+    for distance in range(1, planes - 1):
+        z_stage(0, distance)
+    if chunks > 1:
+        own_sends(1)
 
     def step(k, carry):
-        z_stage(k)
+        z_stage(k, planes - 1)
+        if planes > 2:
+            @pl.when(k + 1 < chunks)
+            def _():
+                z_stage(k + 1, 1)
+
+        @pl.when(k + 2 < chunks)
+        def _():
+            own_sends(k + 2)
+
+        @pl.when(k > 0)
+        def _():
+            relay(k - 1)
+
         load_chunk(k)
         rotate(k)
 
-        @pl.when(k > 0)
-        def _():
-            arrivals(k - 1)
-            gram(k - 1)
+        @pl.when(k + 1 < chunks)
+        def _():
+            for distance in range(2, planes - 1):
+                z_stage(k + 1, distance)
+
+        @pl.when(k > 1)
+        def _():
+            arrivals(k - 2)
+            gram(k - 2)
 
         return carry
 
@@ -257,6 +291,10 @@
     for m in range(1, 8):
         square_copy(m).start()
     last = chunks - 1
+    if chunks > 1:
+        arrivals(last - 1)
+        gram(last - 1)
+    relay(last)
     arrivals(last)
 
     def final(f, carry):
@@ -332,13 +370,15 @@
     wide = 2 * piece
     groups = D // LANES
     spread = LANES // BLOCK
-    inner = jnp.kron(jnp.eye(spread, dtype=jnp.bfloat16), hadamard(BLOCK))
-    outer = jnp.kron(hadamard(spread), jnp.eye(BLOCK, dtype=jnp.bfloat16))
-    picked = jnp.take(row_bank, token_ids, axis=0) * sign_flips.astype(jnp.bfloat16)[None, :]
+    inner = jnp.asarray(np.kron(np.eye(spread), sylvester(BLOCK)), jnp.bfloat16)
+    outer = jnp.asarray(np.kron(sylvester(spread), np.eye(BLOCK)), jnp.bfloat16)
+    signs = sign_flips.astype(jnp.bfloat16)[:, None]
+    picked = jnp.take(row_bank, token_ids, axis=0)
     parts = []
     for g in range(piece):
         part = picked[:, g * LANES : (g + 1) * LANES]
-        part = jnp.dot(part, inner, preferred_element_type=jnp.float32).astype(jnp.bfloat16)
+        table = inner * signs[g * LANES : (g + 1) * LANES]
+        part = jnp.dot(part, table, preferred_element_type=jnp.float32).astype(jnp.bfloat16)
         parts.append(part.reshape(2, chunks, rows, LANES))
     half = jnp.stack(parts, axis=2)
     any_space = pl.BlockSpec(memory_space=pl.ANY)

time: 449 us -> 325 us (0.72)
  Pallas kernels: 410 us -> 294 us
  local copies, waits for them, and re-layouts: 16.3 us -> 11.5 us
    pallas_call x1, Pallas kernels: 410 us -> 294 us  [fused(): pl.pallas_call(functools.partial(fused_kernel, planes, chunks, rows, piec...]
    mul x2 -> x0, local copies, waits for them, and re-layouts: 4.82 us -> none  [the longest x1 2.77 us: fused(): outer = jnp.kron(hadamard(spread), jnp.eye(BLOCK, dtype=jnp.bfloat16))]
where the time goes in v2:
time: 325 us; the launch traced here: 324 us
  Pallas kernels  294 us (90%)
  other arithmetic  15 us (5%)
  local copies, waits for them, and re-layouts  11.5 us (4%)
    pallas_call x1, Pallas kernels, fused(): pl.pallas_call(functools.partial(fused_kernel, planes, chunks, rows, piec...  294 us
    gather x1, local copies, waits for them, and re-layouts, fused(): picked = jnp.take(row_bank, token_ids, axis=0)  11.4 us
    add x1, other arithmetic, damped(): return gram_block + damping[0] * mean_diag * on_diag  10.1 us

profile of v2, /device:TPU:0, one launch (start us, length us, event | category | flops | bytes accessed | tf_op | source)
XLA Modules:
  0.0 324.4 jit_solution(9135410047877539953)
XLA Ops:
  0.0 0.7 compare_select_fusion
  0.7 0.0 copy-start
  0.7 11.4 %gather_fusion = bf16[1536,1024]{1,0:T(8,128)(2,1)S(1)} fusion(bf16[16384,1024]{1,0:T(8,128)(2,1)} %param.6, s32[2048]{0:T(1024)S(1)} %pad_clamp_fusion), kind=kCustom, calls=%fused_computation | custom fusion | bytes 6297600 | tf_op jit(solution)/shard_map/jit(_take)/gather | solution.py:376
  12.1 0.0 copy-done
  12.2 0.0 copy-start.1
  12.2 0.0 copy-start.2
  12.2 0.9 broadcast_select_fusion
  13.1 0.0 copy-done.1
  13.2 0.1 copy-done.2
  13.2 1.1 convolution_convert_fusion.1
  14.3 1.1 convolution_convert_fusion
  15.4 1.9 pad_maximum_fusion.half_ref
  17.3 294.3 %shard_map.64 = (f32[2048,1024]{1,0:T(8,128)}, f32[2048,1024]{1,0:T(8,128)}, f32[16,128]{1,0:T(8,128)}, bf16[12,8,2,64,512]{4,3,2,1,0:T(8,128)(2,1)}) custom-call(bf16[2,12,2,64,512]{4,3,2,1,0:T(8,128)(2,1)} %pad_maximum_fusion.half_ref, bf16[512,512]{1,0:T(8,128)(2,1)} %constant.45.clone.table_ref), custom_call_target="tpu_custom_call" | custom-call | tf_op jit(solution)/shard_map/pallas_call | solution.py:388
  311.6 1.3 reduce_sum.9
  314.2 10.1 %select_add_fusion = f32[2048,1024]{1,0:T(8,128)} fusion(f32[2048,1024]{1,0:T(8,128)} %get-tuple-element.8, f32[2048,1024]{1,0:T(8,128)} %get-tuple-element.9, f32[]{:T(128)S(6)} %mul.37, s32[1024]{0:T(1024)S(1)} %iota_add_fusion.1, s32[2048]{0:T(1024)S(1)} %iota_add_fusion), kind=kLoop, calls=%fused_computation.1 | loop fusion | flops 10485760 | bytes 25178116 | tf_op jit(solution)/shard_map/add | solution.py:433
  (6 shorter events, 0.0 us)
Async XLA Ops:
  0.7 11.4 %copy-start = (s32[1536]{0:T(1024)S(1)}, s32[1536]{0:T(1024)}, u32[]{:S(2)}) copy-start(s32[1536]{0:T(1024)} %param.7) | copy-start | bytes 18436
  12.2 1.0 copy-start.1
  12.2 1.0 copy-start.2
